TPU v7x, 32 devices: a whole 2x2x4 slice. The times are simulated.
32 devices in a mesh: dp: 8 (over z, core), mp: 4 (over y, x).
Axes of the slice: x: 2, y: 2, z: 4, core: 2. Of those that a mesh axis runs over, the one named last changes fastest.
Arguments:
- hidden_states: bfloat16 [32, 640, 1280], P(('dp', 'mp')), may hold values from -6 to 6
- ln_attn_gain: float32 [1280], replicated, may hold values from 0.1 to 1.9
- w_qkv: bfloat16 [1280, 16, 192], P(None, 'mp'), may hold values from -0.15625 to 0.15625
- output_weight: bfloat16 [64, 16, 1280], P(None, 'mp'), may hold values from -0.75 to 0.75
- ln_final_gain: float32 [1280], replicated, may hold values from 0.1 to 1.9
- dense_weight: bfloat16 [1280, 1280], replicated, may hold values from -0.15625 to 0.15625
- decoder_weight: bfloat16 [1280, 33], replicated, may hold values from -0.5390625 to 0.5390625
- decoder_bias: float32 [33], replicated, may hold values from -4 to 4
- seq_tokens: int32 [24, 640], replicated, may hold values from 4 to 23
- seq_lengths: int32 [24], replicated, may hold values from 128 to 640
- copy_sequence: int32 [32], replicated, may hold values from 0 to 23
- mask_code: int32 [32, 64], replicated, may hold values from 0 to 1048575
- copy_owner: int32 [32], replicated, may hold values from 0 to 31, each once
Outputs:
- pll: float32 [32, 64], P('dp', 'mp')
Inputs may be any that keep to these rules, and one draw needn't show every extreme that they name: `seq_tokens`: amino-acid token ids. `copy_owner`: every row of pll is named by exactly one copy.
All inputs are finite; a program needn't handle non-finite values.
Results may differ from a plain program's by a relative error of at most 0.0038.
Values may be sent and summed in bfloat16 or wider, within the bound.
A program may use at most 128 MiB of HBM per device.

v0:
```python
import jax
import jax.numpy as jnp
from jax import lax
from jax.sharding import PartitionSpec as P

epsilon = 1e-05


def layer_norm(inputs):
    average = jnp.mean(inputs, axis=-1, keepdims=True)
    centred = inputs - average
    variance = jnp.mean(centred * centred, axis=-1, keepdims=True)
    return centred * lax.rsqrt(variance + epsilon)


def rotary_tables(seq_span, head_size):
    half_width = head_size // 2
    frequency = 1.0 / 10000.0 ** (jnp.arange(half_width, dtype=jnp.float32) * (2.0 / head_size))
    angles = jnp.arange(seq_span, dtype=jnp.float32)[:, None] * frequency[None, :]
    angles = jnp.concatenate([angles, angles], axis=-1)
    return (jnp.cos(angles), jnp.sin(angles))


def rotate(inputs, cosine, sine):
    half_width = inputs.shape[-1] // 2
    turned = jnp.concatenate([-inputs[..., half_width:], inputs[..., :half_width]], axis=-1)
    return inputs * cosine + turned * sine


def score_rows(residual, ln_final_gain, dense_weight, decoder_weight, decoder_bias, targets):
    feature = residual.shape[-1]
    normed_final = (layer_norm(residual) * ln_final_gain).astype(jnp.bfloat16).reshape(-1, feature)
    dense_out = jnp.dot(normed_final, dense_weight, preferred_element_type=jnp.float32)
    headed = layer_norm(jax.nn.gelu(dense_out, approximate=False)).astype(jnp.bfloat16)
    logits = jnp.dot(headed, decoder_weight, preferred_element_type=jnp.float32) + decoder_bias
    log_probs = logits - jax.nn.logsumexp(logits, axis=-1, keepdims=True)
    vocab_ids = jnp.arange(logits.shape[-1], dtype=jnp.int32)
    flat_targets = targets.reshape(-1)
    picked = jnp.sum(
        jnp.where(flat_targets[:, None] == vocab_ids[None, :], log_probs, 0.0), axis=-1
    )
    return picked.reshape(targets.shape)


def copy_meta(first, amount, tables):
    seq_tokens, seq_lengths, copy_sequence, mask_code = tables
    sequence = lax.dynamic_slice_in_dim(copy_sequence, first, amount, 0)
    codes = lax.dynamic_slice_in_dim(mask_code, first, amount, 0)
    seq_ids = jnp.arange(seq_lengths.shape[0], dtype=jnp.int32)
    lengths = jnp.sum(
        jnp.where(sequence[:, None] == seq_ids[None, :], seq_lengths[None, :], 0), axis=1
    )
    positions = codes % lengths[:, None]
    return (sequence, lengths, positions)


def attend_projected(projected, out_part, lengths, positions, cosine, sine):
    copies, seq_span, head_count, three, head_size = projected.shape
    key_matrix = rotate(
        projected[:, :, :, 1], cosine[None, :, None, :], sine[None, :, None, :]
    ).astype(jnp.bfloat16)
    value_matrix = projected[:, :, :, 2].astype(jnp.bfloat16)
    query_matrix = projected[jnp.arange(copies)[:, None], positions, :, 0] * head_size ** (-0.5)
    query_matrix = rotate(
        query_matrix, cosine[positions][:, :, None, :], sine[positions][:, :, None, :]
    ).astype(jnp.bfloat16)
    attention_logits = jnp.einsum(
        "cmhd,clhd->chml", query_matrix, key_matrix, preferred_element_type=jnp.float32
    )
    alive = jnp.arange(seq_span, dtype=jnp.int32)[None, :] < lengths[:, None]
    attention_logits = jnp.where(alive[:, None, None, :], attention_logits, -1e30)
    largest = jnp.max(attention_logits, axis=-1, keepdims=True)
    weights = jnp.exp(attention_logits - largest)
    attention_probs = (weights / jnp.sum(weights, axis=-1, keepdims=True)).astype(jnp.bfloat16)
    context_vectors = jnp.einsum(
        "chml,clhd->cmhd", attention_probs, value_matrix, preferred_element_type=jnp.float32
    ).astype(jnp.bfloat16)
    return jnp.einsum(
        "cmhd,dhe->cme", context_vectors, out_part, preferred_element_type=jnp.float32
    )


def on_device(
    hidden_states,
    ln_attn_gain,
    w_qkv,
    output_weight,
    ln_final_gain,
    dense_weight,
    decoder_weight,
    decoder_bias,
    seq_tokens,
    seq_lengths,
    copy_sequence,
    mask_code,
    copy_owner,
):
    lane_copies, seq_span, feature = hidden_states.shape
    model_size = lax.axis_size("mp")
    model_index = lax.axis_index("mp")
    group_copies = lane_copies * model_size
    head_size = output_weight.shape[0]
    mask_count = mask_code.shape[1]
    own_masks = mask_count // model_size
    cosine, sine = rotary_tables(seq_span, head_size)
    tables = (seq_tokens, seq_lengths, copy_sequence, mask_code)
    group_first = lax.axis_index("dp") * group_copies
    sequence, lengths, positions = copy_meta(group_first, group_copies, tables)
    targets = jnp.take_along_axis(seq_tokens[sequence], positions, axis=1)
    own_targets = lax.dynamic_slice_in_dim(targets, model_index * own_masks, own_masks, 1)
    lane_start = model_index * lane_copies
    lane_positions = lax.dynamic_slice_in_dim(positions, lane_start, lane_copies, 0)
    normed = (layer_norm(hidden_states.astype(jnp.float32)) * ln_attn_gain).astype(jnp.bfloat16)
    own_rows = hidden_states[jnp.arange(lane_copies)[:, None], lane_positions].astype(jnp.float32)
    lane_lengths = lax.dynamic_slice_in_dim(lengths, lane_start, lane_copies, 0)
    qkv_part = lax.all_gather(w_qkv, "mp", axis=1, tiled=True)
    out_part = lax.all_gather(output_weight, "mp", axis=1, tiled=True)
    count = qkv_part.shape[1]
    made = jnp.dot(
        normed.reshape(-1, feature),
        qkv_part.reshape(feature, -1),
        preferred_element_type=jnp.float32,
    )
    made = made.reshape(lane_copies, seq_span, count, 3, head_size)
    attention_mixed = attend_projected(made, out_part, lane_lengths, lane_positions, cosine, sine)
    lane_rows = own_rows + attention_mixed
    residual = lax.all_to_all(lane_rows, "mp", split_axis=1, concat_axis=0, tiled=True)
    attention_logits = score_rows(
        residual, ln_final_gain, dense_weight, decoder_weight, decoder_bias, own_targets
    )
    everything = lax.all_gather(attention_logits, "dp", axis=0, tiled=True)
    wanted = group_first + jnp.arange(group_copies, dtype=jnp.int32)
    copy_ids = jnp.arange(copy_owner.shape[0], dtype=jnp.int32)
    source = jnp.sum(
        jnp.where(copy_owner[None, :] == wanted[:, None], copy_ids[None, :], 0), axis=1
    )
    return everything[source]


def solution(mesh):
    placed = (
        P(("dp", "mp"), None, None),
        P(),
        P(None, "mp", None),
        P(None, "mp", None),
        P(),
        P(),
        P(),
        P(),
        P(),
        P(),
        P(),
        P(),
        P(),
    )
    return jax.shard_map(
        on_device, mesh=mesh, in_specs=placed, out_specs=P("dp", "mp"), check_vma=False
    )
```

profile of v0, /device:TPU:0, one launch (start us, length us, event | category | flops | bytes accessed | tf_op | source)
XLA Modules:
  0.0 182.3 jit_solution(14056462352074514174)
XLA Ops:
  7.3 2.1 %copy.38 = bf16[64,4,1280]{2,0,1:T(8,128)(2,1)} copy(bf16[64,4,1280]{2,1,0:T(4,128)(2,1)} %param.16) | data formatting | bytes 1310720 | tf_op args[3]
  11.5 1.7 convert_reduce_fusion
  13.9 2.1 %fusion.52 = (f32[640,64]{1,0:T(8,128)}, f32[640,64]{1,0:T(8,128)}) fusion(f32[640,32]{1,0:T(8,128)S(1)} %iota_multiply_fusion), kind=kLoop, calls=%fused_computation.81 | loop fusion | flops 40960 | bytes 409600 | tf_op jit(solution)/shard_map/cos | solution.py:21
  16.7 2.5 %gather_fusion.6 = s32[256]{0:T(256)S(1)} fusion(s32[4,640]{1,0:T(4,128)S(1)} %gather_fusion, s32[256]{0:T(256)S(1)} %reshape.339), kind=kCustom, calls=%fused_computation.6 | custom fusion | bytes 4096 | tf_op jit(solution)/shard_map/jit(take_along_axis)/gather | solution.py:109
  20.7 1.2 copy.35
  21.9 1.7 gather_fusion.3
  23.5 1.6 gather_fusion.4
  25.1 1.8 copy.36
  26.9 2.5 %gather_fusion.1 = bf16[64,1280]{1,0:T(8,128)(2,1)} fusion(bf16[1,640,1280]{2,1,0:T(8,128)(2,1)} %param.13, s32[64]{0:T(128)S(1)} %or_bitcast_fusion.1), kind=kCustom, calls=%fused_computation.1 | custom fusion | bytes 328192 | tf_op jit(solution)/shard_map/gather | solution.py:114
  30.1 65.0 %all-gather.4.cloned.1.call-done = bf16[1280,16,192]{0,2,1:T(8,128)(2,1)} async-done(((bf16[1280,4,192]{0,2,1:T(8,128)(2,1)}), bf16[1280,16,192]{0,2,1:T(8,128)(2,1)}) %all-gather.4.cloned.1.call-update) | async-done | bytes 7864336 | tf_op jit(solution)/shard_map/all_gather | solution.py:116
  95.1 11.3 %convolution_bitcast_fusion = f32[1,640,16,3,64]{1,4,3,2,0:T(8,128)} fusion(bf16[16,3,64,1280]{3,2,1,0:T(8,128)(2,1)} %bitcast.96, bf16[1,640,1280]{2,1,0:T(8,128)(2,1)} %param.13, f32[1280]{0:T(1024)S(1)} %copy-done.10, f32[640]{0:T(1024)S(1)} %add_rsqrt_fusion, f32[640]{0:T(1024)S(1)} %broadcast_multiply_fusion.1), kind=kOutput, calls=%fused_computation.15 | convolution fusion | flops 5037260800 | bytes 17377280 | tf_op jit(solution)/shard_map/dot_general | solution.py:119
  106.4 15.1 %copy.34 = f32[1,640,16,3,64]{4,2,3,1,0:T(8,128)} copy(f32[1,640,16,3,64]{1,4,3,2,0:T(8,128)} %convolution_bitcast_fusion) | data formatting | bytes 15728640 | tf_op jit(solution)/shard_map/dot_general | solution.py:119
  121.5 7.0 %gather_fusion.2 = f32[64,16,64]{2,1,0:T(8,128)} fusion(f32[1,640,16,3,64]{4,2,3,1,0:T(8,128)} %copy.34, s32[64]{0:T(128)S(1)} %or_bitcast_fusion), kind=kCustom, calls=%fused_computation.2 | custom fusion | bytes 525056 | tf_op jit(solution)/shard_map/gather | solution.py:63
  130.0 1.9 %slice_bitcast_fusion = f32[1,640,16,64]{1,3,2,0:T(8,128)S(1)} fusion(f32[1,640,16,3,64]{1,4,3,2,0:T(8,128)} %convolution_bitcast_fusion), kind=kLoop, calls=%fused_computation.23 | loop fusion | bytes 5242880 | tf_op jit(solution)/shard_map/squeeze | solution.py:60
  132.9 2.6 %fusion.18 = f32[16,64,640]{2,1,0:T(8,128)S(1)} fusion(f32[640,16,32]{0,2,1:T(8,128)S(1)} %get-tuple-element.10, f32[640,16,32]{0,2,1:T(8,128)S(1)} %get-tuple-element.9, f32[1,640,16,3,64]{1,4,3,2,0:T(8,128)} %convolution_bitcast_fusion, f32[640,64]{0,1:T(8,128)S(1)} %copy-done.3, f32[640,64]{0,1:T(8,128)S(1)} %copy.35, bf16[64,16,64]{2,1,0:T(8,128)(2,1)S(1)} %fusion.38), kind=kOutput, calls=%fused_computation.33 | convolution fusion | flops 87162880 | bytes 8323072 | tf_op jit(solution)/shard_map/cmhd,clhd->chml/dot_general | solution.py:67
  135.5 2.1 %fusion.66 = (f32[16,64]{1,0:T(8,128)S(1)}, f32[16,64,640]{2,1,0:T(8,128)}) fusion(f32[16,64,640]{2,1,0:T(8,128)S(1)} %fusion.18, pred[640]{0:T(1024)(128)(4,1)S(1)} %iota_compare_fusion.1), kind=kOutput, calls=%fused_computation.129 | output fusion | flops 2622079 | bytes 5247616 | tf_op jit(solution)/shard_map/sub | solution.py:73
  137.6 5.1 %fusion.9 = f32[1,64,1280]{2,1,0:T(8,128)} fusion(bf16[64,16,1280]{2,0,1:T(8,128)(2,1)} %all-gather.6.cloned.1.call-done, f32[16,64,640]{2,1,0:T(8,128)} %get-tuple-element.16, f32[16,64]{1,0:T(8,128)S(1)} %get-tuple-element.15, f32[1,640,16,3,64]{1,4,3,2,0:T(8,128)} %convolution_bitcast_fusion, bf16[64,1280]{1,0:T(8,128)(2,1)S(1)} %copy-done.4), kind=kOutput, calls=%fused_computation.26 | convolution fusion | flops 253198336 | bytes 7049216 | tf_op jit(solution)/shard_map/cmhd,dhe->cme/dot_general | solution.py:78
  142.8 2.0 %copy.40 = f32[1,64,1280]{2,0,1:T(1,128)} copy(f32[1,64,1280]{2,1,0:T(8,128)} %fusion.9) | data formatting | bytes 655360 | tf_op jit(solution)/shard_map/add | solution.py:126
  144.8 4.3 %all-to-all-start = ((f32[1,64,1280]{2,0,1:T(1,128)}), f32[1,64,1280]{2,0,1:T(1,128)}, u32[]{:S(2)}, u32[]{:S(2)}) async-start(f32[1,64,1280]{2,0,1:T(1,128)} %copy.40), calls=%async_computation | async-start | bytes 655360 | tf_op jit(solution)/shard_map/all_to_all | solution.py:127
  149.1 5.8 %all-to-all-done = f32[1,64,1280]{2,0,1:T(1,128)} async-done(((f32[1,64,1280]{2,0,1:T(1,128)}), f32[1,64,1280]{2,0,1:T(1,128)}, u32[]{:S(2)}, u32[]{:S(2)}) %all-to-all-start) | async-done | bytes 327712 | tf_op jit(solution)/shard_map/all_to_all | solution.py:127
  154.9 1.5 reduce_sum.105
  156.5 2.0 %multiply_reduce_fusion.1 = f32[64]{0:T(128)S(1)} fusion(f32[1,64,1280]{2,0,1:T(1,128)} %all-to-all-done, f32[64]{0:T(128)S(1)} %broadcast_multiply_fusion.3), kind=kLoop, calls=%fused_computation.76 | loop fusion | flops 245696 | bytes 328192 | tf_op jit(solution)/shard_map/reduce_sum | solution.py:12
  158.5 2.3 %fusion.67 = (f32[64]{0:T(128)S(1)}, f32[64,1280]{1,0:T(8,128)S(1)}) fusion(bf16[1280,1280]{1,0:T(8,128)(2,1)S(1)} %copy-done, f32[1,64,1280]{2,0,1:T(1,128)} %all-to-all-done, f32[1280]{0:T(1024)S(1)} %copy-done.11, f32[64]{0:T(128)S(1)} %add_rsqrt_fusion.2, f32[64]{0:T(128)S(1)} %broadcast_multiply_fusion.3), kind=kOutput, calls=%fused_computation.130 | convolution fusion | flops 215367616 | bytes 3938048 | tf_op jit(solution)/shard_map/dot_general | solution.py:33
  161.5 12.8 %all-gather = f32[8,4,16]{2,1,0:T(4,128)S(1)} all-gather(f32[1,4,16]{2,1,0:T(4,128)S(1)} %reshape.362), channel_id=1, replica_groups=mesh['dp'=8,'mp'=4] {'dp'}, dimensions={0}, use_global_device_ids=true | all-gather | bytes 2304 | tf_op jit(solution)/shard_map/all_gather | solution.py:131
  (83 shorter events, 10.6 us)
Async XLA Ops:
  6.5 152.0 %copy-start = (bf16[1280,1280]{1,0:T(8,128)(2,1)S(1)}, bf16[1280,1280]{1,0:T(8,128)(2,1)}, u32[]{:S(2)}) copy-start(bf16[1280,1280]{1,0:T(8,128)(2,1)} %param.18) | copy-start | bytes 9830404
  6.5 2.9 %copy-start.9 = (s32[32]{0:T(128)S(1)}, s32[32]{0:T(128)}, u32[]{:S(2)}) copy-start(s32[32]{0:T(128)} %param.23) | copy-start | bytes 388
  6.5 3.0 %copy-start.12 = (s32[24]{0:T(128)S(1)}, s32[24]{0:T(128)}, u32[]{:S(2)}) copy-start(s32[24]{0:T(128)} %param.22) | copy-start | bytes 292
  6.5 88.5 %all-gather.4.cloned.1.call-start = ((), (), s32[]{:S(2)}) async-start(), calls=%async_computation.1 | async-start | bytes 9830400 | tf_op jit(solution)/shard_map/all_gather | solution.py:116
  7.3 130.4 %all-gather.6.cloned.1.call-start = ((), (), s32[]{:S(2)}) async-start(), calls=%async_computation.2 | async-start | bytes 3276800 | tf_op jit(solution)/shard_map/all_gather | solution.py:117
  9.4 6.7 %copy-start.6 = (s32[24,640]{1,0:T(8,128)S(1)}, s32[24,640]{1,0:T(8,128)}, u32[]{:S(2)}) copy-start(s32[24,640]{1,0:T(8,128)} %param.21) | copy-start | bytes 184324
  9.8 3.4 %copy-start.1 = (bf16[1,640,1280]{2,1,0:T(8,128)(2,1)S(1)}, bf16[1,640,1280]{2,1,0:T(8,128)(2,1)}, u32[]{:S(2)}) copy-start(bf16[1,640,1280]{2,1,0:T(8,128)(2,1)} %param.13) | copy-start | bytes 4915204
  13.2 6.1 %copy-start.13 = (s32[32]{0:T(128)S(1)}, s32[32]{0:T(128)}, u32[]{:S(2)}) copy-start(s32[32]{0:T(128)} %param.25) | copy-start | bytes 388
  16.7 78.4 %copy-start.10 = (f32[1280]{0:T(1024)S(1)}, f32[1280]{0:T(1024)}, u32[]{:S(2)}) copy-start(f32[1280]{0:T(1024)} %param.14) | copy-start | bytes 15364
  121.5 8.3 %copy-start.5 = (f32[64,64]{1,0:T(8,128)S(1)}, f32[64,64]{1,0:T(8,128)}, u32[]{:S(2)}) copy-start(f32[64,64]{1,0:T(8,128)} %broadcast_multiply_fusion) | copy-start | bytes 49156
  128.4 1.4 copy-start.2
  132.0 0.9 copy-start.3
  135.5 2.1 %copy-start.4 = (bf16[64,1280]{1,0:T(8,128)(2,1)S(1)}, bf16[64,1280]{1,0:T(8,128)(2,1)}, u32[]{:S(2)}) copy-start(bf16[64,1280]{1,0:T(8,128)(2,1)} %gather_fusion.1) | copy-start | bytes 491524
  137.6 11.4 %copy-start.14 = (s32[4]{0:T(128)S(1)}, s32[4]{0:T(128)}, u32[]{:S(2)}) copy-start(s32[4]{0:T(128)} %select_reduce_fusion.2) | copy-start | bytes 52
  137.6 20.9 %copy-start.11 = (f32[1280]{0:T(1024)S(1)}, f32[1280]{0:T(1024)}, u32[]{:S(2)}) copy-start(f32[1280]{0:T(1024)} %param.17) | copy-start | bytes 15364
  144.8 10.2 %all-to-all-start = ((f32[1,64,1280]{2,0,1:T(1,128)}), f32[1,64,1280]{2,0,1:T(1,128)}, u32[]{:S(2)}, u32[]{:S(2)}) async-start(f32[1,64,1280]{2,0,1:T(1,128)} %copy.40), calls=%async_computation | async-start | bytes 655360 | tf_op jit(solution)/shard_map/all_to_all | solution.py:127
  158.5 2.6 %copy-start.7 = (bf16[1280,33]{0,1:T(8,128)(2,1)S(1)}, bf16[1280,33]{0,1:T(8,128)(2,1)}, u32[]{:S(2)}) copy-start(bf16[1280,33]{0,1:T(8,128)(2,1)} %param.19) | copy-start | bytes 253444
  158.5 2.6 %copy-start.8 = (f32[33]{0:T(128)S(1)}, f32[33]{0:T(128)}, u32[]{:S(2)}) copy-start(f32[33]{0:T(128)} %param.20) | copy-start | bytes 400
Sparse Core Ops, SparseCore 0:
  9.2 85.8 all-gather.3
  96.9 39.4 all-gather.5
where the time goes:
time: 183 us; the launch traced here: 182 us
  waiting for transfers between devices  71.5 us (39%)
  local copies, waits for them, and re-layouts  42.8 us (23%)
  matrix products  21.6 us (12%)
  other arithmetic  15.5 us (8%)
  between operations  13.7 us (7%)
  blocking collectives  12.8 us (7%)
  starting transfers between devices  4.32 us (2%)
    all_gather x1, waiting for transfers between devices, on_device(): qkv_part = lax.all_gather(w_qkv, 'mp', axis=1, tiled=True)  65 us
    dot_general x1, local copies, waits for them, and re-layouts, on_device(): jnp.dot(normed.reshape(-1, feature), qkv_part.reshape(feature, -1), prefe...  15.1 us
    all_gather x1, blocking collectives, on_device(): everything = lax.all_gather(attention_logits, 'dp', axis=0, tiled=True)  12.8 us
    dot_general x1, matrix products, on_device(): jnp.dot(normed.reshape(-1, feature), qkv_part.reshape(feature, -1), prefe...  11.3 us
    gather x1, local copies, waits for them, and re-layouts, attend_projected(): projected[jnp.arange(copies)[:, None], positions, :, 0]  6.96 us
    all_to_all x1, waiting for transfers between devices, on_device(): lax.all_to_all(lane_rows, 'mp', split_axis=1, concat_axis=0, tiled=True)  5.85 us
    dot_general x1, matrix products, attend_projected(): jnp.einsum('cmhd,dhe->cme', context_vectors, out_part, preferred_element_...  5.14 us
    all_to_all x1, starting transfers between devices, on_device(): lax.all_to_all(lane_rows, 'mp', split_axis=1, concat_axis=0, tiled=True)  4.28 us
  transfers between devices with their start and end apart: 3, of which 2 were waited for; matrix products, arithmetic and copies ran while one was open for 35% of the time, Pallas kernels for 0%

commit v1 on v0

v1 whole, which is shorter than its diff:
```python
import functools

import jax
import jax.numpy as jnp
import numpy as np
from jax import lax
from jax.experimental import pallas as pl
from jax.experimental.pallas import tpu as pltpu
from jax.sharding import PartitionSpec as P

epsilon = 1e-05
MESH = pl.DeviceIdType.MESH
f32 = jnp.float32
bf16 = jnp.bfloat16
LANES = 128


def layer_norm(inputs):
    average = jnp.mean(inputs, axis=-1, keepdims=True)
    centred = inputs - average
    variance = jnp.mean(centred * centred, axis=-1, keepdims=True)
    return centred * lax.rsqrt(variance + epsilon)


def rotary_tables(seq_span, head_size):
    half = head_size // 2
    frequency = (1.0 / 10000.0 ** (np.arange(half, dtype=np.float32) * (2.0 / head_size))).astype(
        np.float32
    )
    angles = np.arange(seq_span, dtype=np.float32)[:, None] * frequency[None, :]
    cosine, sine = np.cos(angles), np.sin(angles)
    times = LANES // head_size
    return (
        np.tile(np.concatenate([cosine, cosine], axis=1), (1, times)).astype(np.float32),
        np.tile(np.concatenate([-sine, sine], axis=1), (1, times)).astype(np.float32),
    )


def flip(index, mask):
    bit = 1
    out = index
    while bit <= mask:
        if mask & bit:
            out = out + bit * (1 - 2 * ((index // bit) % 2))
        bit *= 2
    return out


def kernel(
    sizes,
    sequence_ref,
    lengths_ref,
    codes_ref,
    tokens_ref,
    owner_ref,
    gain_ref,
    final_gain_ref,
    decoder_ref,
    bias_ref,
    hidden_hbm,
    weight_hbm,
    out_weight_hbm,
    dense_hbm,
    cos_hbm,
    sin_hbm,
    out_ref,
    hidden,
    normed,
    wbuf,
    obuf,
    dense,
    cos,
    sin,
    pbuf,
    context,
    mixed,
    scores,
    local_sem,
    direct_sem,
    relay_sem,
    share_sem,
    arrive_sem,
    shared_sem,
    score_send_sem,
    score_sem,
):
    n_dp, n_mp, head_size, heads_in_chunk, chunks = sizes
    devices = n_dp * n_mp
    dp = lax.axis_index("dp")
    mp = lax.axis_index("mp")
    core = dp % 2
    partner = dp + 1 - 2 * core
    me = dp * n_mp + mp
    seq_span, feature = hidden.shape
    masks = codes_ref.shape[1]
    chunk_rows = chunk_heads = heads_in_chunk * head_size
    half_rows = feature // 2
    out_rows = obuf.shape[1]
    piece_rows = out_rows // 4

    def local(index, source, target):
        copy = pltpu.make_async_copy(source, target, local_sem.at[index])
        copy.start()
        return copy

    hidden_copy = local(0, hidden_hbm, hidden)
    weight_copy = local(1, weight_hbm, wbuf.at[0])
    out_weight_copy = local(2, out_weight_hbm, obuf.at[0])
    cos_copy = local(3, cos_hbm, cos)
    sin_copy = local(4, sin_hbm, sin)
    dense_copy = local(5, dense_hbm, dense)

    barrier = pltpu.get_barrier_semaphore()

    def greet(step, carry):
        other = (me + step) % devices
        pl.semaphore_signal(
            barrier, inc=1, device_id=(other // n_mp, other % n_mp), device_id_type=MESH
        )
        return carry

    lax.fori_loop(1, devices, greet, 0)

    def view(relation, item):
        if item < chunks:
            return wbuf.at[relation, item, pl.ds(pl.multiple_of(core * half_rows, 16), half_rows), :]
        start = core * (2 * piece_rows) + (item - chunks) * piece_rows
        return obuf.at[relation, pl.ds(pl.multiple_of(start, 16), piece_rows), :]

    def partner_view(relation, item):
        if item < chunks:
            start = (1 - core) * half_rows
            return wbuf.at[relation, item, pl.ds(pl.multiple_of(start, 16), half_rows), :]
        start = (1 - core) * (2 * piece_rows) + (item - chunks) * piece_rows
        return obuf.at[relation, pl.ds(pl.multiple_of(start, 16), piece_rows), :]

    sent = []

    def to_group(target, source_relation, relation, item, semaphore):
        copy = pltpu.make_async_remote_copy(
            src_ref=view(source_relation, item),
            dst_ref=view(relation, item),
            send_sem=semaphore,
            recv_sem=arrive_sem.at[relation, item],
            device_id=(dp, flip(mp, target)),
            device_id_type=MESH,
        )
        copy.start()
        sent.append(copy)

    def direct(target, item):
        to_group(target, 0, target, item, direct_sem.at[target, item])

    def relay(target, source_relation, item):
        to_group(target, source_relation, source_relation ^ target, item, relay_sem.at[item])

    def arrived(relation, item):
        landing = view(relation, item)
        pltpu.make_async_copy(landing, landing, arrive_sem.at[relation, item]).wait()

    def share(relation, item):
        copy = pltpu.make_async_remote_copy(
            src_ref=view(relation, item),
            dst_ref=view(relation, item),
            send_sem=share_sem.at[relation, item],
            recv_sem=shared_sem.at[relation, item],
            device_id=(partner, mp),
            device_id_type=MESH,
        )
        copy.start()
        sent.append(copy)

    def was_shared(relation, item):
        landing = partner_view(relation, item)
        pltpu.make_async_copy(landing, landing, shared_sem.at[relation, item]).wait()

    sequence = sequence_ref[me]
    length = lengths_ref[sequence].astype(f32)
    codes = codes_ref[pl.ds(me, 1), :].astype(f32)
    quotient = jnp.floor(codes / length)
    row_positions = codes - quotient * length
    row_positions = jnp.where(row_positions < 0.0, row_positions + length, row_positions)
    row_positions = jnp.where(row_positions >= length, row_positions - length, row_positions)
    eye = lax.broadcasted_iota(jnp.int32, (masks, masks), 0) == lax.broadcasted_iota(
        jnp.int32, (masks, masks), 1
    )
    positions = jnp.sum(jnp.where(eye, row_positions, 0.0), axis=1, keepdims=True)
    places = lax.broadcasted_iota(jnp.int32, (masks, seq_span), 1).astype(f32)
    chosen = places == positions
    onehot = jnp.where(chosen, 1.0, 0.0)
    onehot_bf = onehot.astype(bf16)
    tokens = tokens_ref[pl.ds(sequence, 1), :].astype(f32)
    targets = jnp.sum(jnp.where(chosen, tokens, 0.0), axis=1, keepdims=True)
    alive = lax.broadcasted_iota(jnp.int32, (1, seq_span), 1).astype(f32) < length

    weight_copy.wait()
    out_weight_copy.wait()
    pl.semaphore_wait(barrier, devices - 1)
    items = chunks + 2
    routed = n_mp == 4 and chunks == 2
    if routed:
        direct(1, 0)
        direct(2, 1)
        direct(1, 1)
        direct(2, 0)
    else:
        for item in range(items):
            for target in range(1, n_mp):
                direct(target, item)

    hidden_copy.wait()
    tile = 128 if seq_span % 128 == 0 else 8

    def norm_rows(step, carry):
        rows = pl.ds(pl.multiple_of(step * tile, tile), tile)
        normed[rows, :] = (layer_norm(hidden[rows, :].astype(f32)) * gain_ref[...]).astype(bf16)
        return carry

    lax.fori_loop(0, seq_span // tile, norm_rows, 0)
    masked_rows = jnp.dot(onehot_bf, normed[...], preferred_element_type=f32).astype(bf16)
    own_rows = jnp.dot(onehot_bf, hidden[...], preferred_element_type=f32)
    mixed[...] = own_rows
    cos_copy.wait()
    sin_copy.wait()
    exact = dict(preferred_element_type=f32, precision=lax.Precision.HIGHEST)
    query_cos = jnp.dot(onehot, cos[...], **exact)
    query_sin = jnp.dot(onehot, sin[...], **exact)
    lane = lax.broadcasted_iota(jnp.int32, (1, LANES), 1)
    first = lane % head_size < head_size // 2

    def rotate(inputs, cosine, sine):
        turned = jnp.where(
            first,
            pltpu.roll(inputs, LANES - head_size // 2, 1),
            pltpu.roll(inputs, head_size // 2, 1),
        )
        return inputs * cosine + turned * sine

    width = wbuf.shape[3]
    span = seq_span // 2 if seq_span % 32 == 0 else seq_span

    def attend(relation, chunk):
        weights = wbuf.at[relation, chunk]

        def project(step, carry):
            rows = pl.ds(pl.multiple_of(step * span, 16), span)
            made = jnp.dot(normed[rows, :], weights[...], preferred_element_type=f32)
            for start in range(0, width, LANES):
                end = min(start + LANES, width)
                part = made[:, start:end]
                keys = [
                    head * 3 * head_size + head_size
                    for head in range(heads_in_chunk)
                    if start <= head * 3 * head_size + head_size < end
                ]
                for key in keys:
                    low = key - start
                    turned = rotate(part, cos[rows, :], sin[rows, :])
                    inside = (lane >= low) & (lane < low + head_size)
                    part = jnp.where(inside, turned, part)
                pbuf[rows, start:end] = part.astype(bf16)
            return carry

        lax.fori_loop(0, seq_span // span, project, 0)
        made = jnp.dot(masked_rows, weights[...], preferred_element_type=f32) * head_size ** (-0.5)
        total = None
        for head in range(heads_in_chunk):
            at = head * 3 * head_size
            block = at // LANES * LANES
            query = rotate(made[:, block : block + LANES], query_cos, query_sin)
            query = pltpu.roll(query, head_size, 1)
            key = at + head_size
            block = key // LANES * LANES
            inside = (lane >= key - block) & (lane < key - block + head_size)
            query = jnp.where(inside, query, 0.0).astype(bf16)
            logits = lax.dot_general(
                query,
                pbuf[:, block : block + LANES],
                (((1,), (1,)), ((), ())),
                preferred_element_type=f32,
            )
            logits = jnp.where(alive, logits, -1e30)
            weight = jnp.exp(logits - jnp.max(logits, axis=-1, keepdims=True))
            probs = (weight / jnp.sum(weight, axis=-1, keepdims=True)).astype(bf16)
            value = at + 2 * head_size
            block = value // LANES * LANES
            end = min(block + LANES, width)
            vectors = jnp.dot(probs, pbuf[:, block:end], preferred_element_type=f32)
            if total is None:
                total = vectors
            else:
                low = value - block
                inside = (lane >= low) & (lane < low + head_size)
                total = jnp.where(inside, vectors, total)
        context[relation, chunk] = total.astype(bf16)

    def mix(relation):
        for chunk in range(chunks):
            rows = slice(chunk * chunk_heads, (chunk + 1) * chunk_heads)
            mixed[...] += jnp.dot(
                context[relation, chunk], obuf[relation, rows, :], preferred_element_type=f32
            )

    def attend_all(pairs):
        for relation, chunk in pairs:
            attend(relation, chunk)

    attend_all([(0, chunk) for chunk in range(chunks)])
    mix(0)

    def fetch(pairs, relays=()):
        for pair in pairs:
            arrived(*pair)
            for target, source_relation, item in relays:
                if (source_relation, item) == pair:
                    relay(target, source_relation, item)
            share(*pair)

    if routed:
        relays = [(1, 2, 1), (2, 1, 0), (1, 2, chunks + 1), (2, 1, chunks)]
        fetch([(1, 0), (2, 1)], relays)
        for item in (chunks, chunks + 1):
            direct(1, 2 * chunks + 1 - item)
            direct(2, item)
        for pair in [(1, 0), (2, 1)]:
            was_shared(*pair)
            attend(*pair)
        fetch([(1, 1), (2, 0)], relays)
        for pair in [(1, 1), (2, 0)]:
            was_shared(*pair)
            attend(*pair)
        fetch([(3, 0), (3, 1)])
        for pair in [(3, 0), (3, 1)]:
            was_shared(*pair)
            attend(*pair)
        fetch([(1, chunks), (2, chunks + 1), (1, chunks + 1), (2, chunks)], relays)
        fetch([(3, chunks), (3, chunks + 1)])
        for relation in (1, 2, 3):
            was_shared(relation, chunks)
            was_shared(relation, chunks + 1)
            mix(relation)
    else:
        for relation in range(1, n_mp):
            fetch([(relation, item) for item in range(items)])
        for relation in range(1, n_mp):
            for item in range(items):
                was_shared(relation, item)
            attend_all([(relation, chunk) for chunk in range(chunks)])
            mix(relation)

    normed_final = (layer_norm(mixed[...]) * final_gain_ref[...]).astype(bf16)
    dense_copy.wait()
    dense_out = jnp.dot(normed_final, dense[...], preferred_element_type=f32)
    headed = layer_norm(0.5 * dense_out * (1.0 + lax.erf(dense_out * 0.5**0.5))).astype(bf16)
    logits = jnp.dot(headed, decoder_ref[...], preferred_element_type=f32) + bias_ref[...]
    largest = jnp.max(logits, axis=-1, keepdims=True)
    scale = jnp.log(jnp.sum(jnp.exp(logits - largest), axis=-1, keepdims=True)) + largest
    vocabulary = lax.broadcasted_iota(jnp.int32, logits.shape, 1).astype(f32)
    picked = jnp.sum(jnp.where(vocabulary == targets, logits - scale, 0.0), axis=1, keepdims=True)
    row = jnp.sum(jnp.where(eye, picked, 0.0), axis=0, keepdims=True)
    padded = jnp.concatenate([row, jnp.zeros((1, LANES - masks), f32)], axis=1) if masks < LANES else row
    scores[me] = jnp.broadcast_to(padded, scores.shape[1:])

    def score_copy(step):
        other = (me + step) % devices
        return pltpu.make_async_remote_copy(
            src_ref=scores.at[me],
            dst_ref=scores.at[me],
            send_sem=score_send_sem.at[step],
            recv_sem=score_sem.at[me],
            device_id=(other // n_mp, other % n_mp),
            device_id_type=MESH,
        )

    def send_scores(step, carry):
        score_copy(step).start()
        return carry

    lax.fori_loop(1, devices, send_scores, 0)
    for copy in sent:
        copy.wait_send()

    def wait_scores(step, carry):
        source = (me + step) % devices
        landing = scores.at[source]
        pltpu.make_async_copy(landing, landing, score_sem.at[source]).wait()
        return carry

    lax.fori_loop(1, devices, wait_scores, 0)

    def wait_sends(step, carry):
        score_copy(step).wait_send()
        return carry

    lax.fori_loop(1, devices, wait_sends, 0)
    group = out_ref.shape[0]
    wanted = dp * group + lax.broadcasted_iota(jnp.int32, (group, owner_ref.shape[1]), 0)
    select = jnp.where(owner_ref[...] == wanted, 1.0, 0.0)
    out_ref[...] = jnp.dot(select, scores[:, 0, :], **exact)


def on_device(
    shape,
    hidden_states,
    ln_attn_gain,
    w_qkv,
    output_weight,
    ln_final_gain,
    dense_weight,
    decoder_weight,
    decoder_bias,
    seq_tokens,
    seq_lengths,
    copy_sequence,
    mask_code,
    copy_owner,
):
    n_dp, n_mp = shape
    devices = n_dp * n_mp
    lane_copies, seq_span, feature = hidden_states.shape
    head_size, heads, _ = output_weight.shape
    copies, masks = mask_code.shape
    assert lane_copies == 1 and copies == devices and n_dp % 2 == 0
    in_chunk = 2 if heads % 2 == 0 else 1
    chunks = heads // in_chunk
    width = in_chunk * 3 * head_size
    weight = jnp.swapaxes(w_qkv.reshape(feature, chunks, width), 0, 1)
    out_weight = jnp.swapaxes(output_weight, 0, 1).reshape(heads * head_size, feature)
    cosine, sine = rotary_tables(seq_span, head_size)
    group = copies // n_dp
    items = chunks + 2
    dma = pltpu.SemaphoreType.DMA
    vmem = pl.BlockSpec(memory_space=pltpu.VMEM)
    smem = pl.BlockSpec(memory_space=pltpu.SMEM)
    anywhere = pl.BlockSpec(memory_space=pl.ANY)
    rows = pl.pallas_call(
        functools.partial(kernel, (n_dp, n_mp, head_size, in_chunk, chunks)),
        name="score_copies",
        out_shape=jax.ShapeDtypeStruct((group, LANES), f32),
        in_specs=[smem] * 2 + [vmem] * 7 + [anywhere] * 6,
        out_specs=vmem,
        scratch_shapes=[
            pltpu.VMEM((seq_span, feature), bf16),
            pltpu.VMEM((seq_span, feature), bf16),
            pltpu.VMEM((n_mp, chunks, feature, width), bf16),
            pltpu.VMEM((n_mp, heads * head_size, feature), bf16),
            pltpu.VMEM((feature, feature), bf16),
            pltpu.VMEM((seq_span, LANES), f32),
            pltpu.VMEM((seq_span, LANES), f32),
            pltpu.VMEM((seq_span, width), bf16),
            pltpu.VMEM((n_mp, chunks, masks, in_chunk * head_size), bf16),
            pltpu.VMEM((masks, feature), f32),
            pltpu.VMEM((devices, 8, LANES), f32),
            dma((6,)),
            dma((n_mp, items)),
            dma((items,)),
            dma((n_mp, items)),
            dma((n_mp, items)),
            dma((n_mp, items)),
            dma((devices,)),
            dma((devices,)),
        ],
        compiler_params=pltpu.CompilerParams(collective_id=0, has_side_effects=True),
    )(
        copy_sequence,
        seq_lengths,
        mask_code,
        seq_tokens,
        copy_owner.reshape(1, -1),
        ln_attn_gain.reshape(1, -1),
        ln_final_gain.reshape(1, -1),
        decoder_weight,
        decoder_bias.reshape(1, -1),
        hidden_states.reshape(seq_span, feature),
        weight,
        out_weight,
        dense_weight,
        jnp.asarray(cosine),
        jnp.asarray(sine),
    )
    own = masks // n_mp
    return lax.dynamic_slice_in_dim(rows, lax.axis_index("mp") * own, own, 1)


def solution(mesh):
    placed = (
        P(("dp", "mp"), None, None),
        P(),
        P(None, "mp", None),
        P(None, "mp", None),
        P(),
        P(),
        P(),
        P(),
        P(),
        P(),
        P(),
        P(),
        P(),
    )
    shape = (mesh.shape["dp"], mesh.shape["mp"])
    return jax.shard_map(
        functools.partial(on_device, shape),
        mesh=mesh,
        in_specs=placed,
        out_specs=P("dp", "mp"),
        check_vma=False,
    )
```

time: 183 us -> 75.1 us (0.41)
  waiting for transfers between devices: 71.5 us -> 0 us
  Pallas kernels: 0 us -> 64 us
  local copies, waits for them, and re-layouts: 42.8 us -> 10.7 us
  matrix products: 21.6 us -> 0 us
  other arithmetic: 15.5 us -> 0 us
  between operations: 13.7 us -> 0.02 us
  blocking collectives: 12.8 us -> 0 us
  starting transfers between devices: 4.32 us -> 0 us
    all_gather x2 -> x0, waiting for transfers between devices: 65 us -> none  [the longest x1 65 us: on_device(): qkv_part = lax.all_gather(w_qkv, 'mp', axis=1, tiled=True)]
    pallas_call x0 -> x1, Pallas kernels: none -> 64 us  [on_device(): pl.pallas_call(functools.partial(kernel, (n_dp, n_mp, head_size, in_chunk...]
    dot_general x5 -> x0, matrix products: 21.6 us -> none  [the longest x1 11.3 us: on_device(): jnp.dot(normed.reshape(-1, feature), qkv_part.reshape(feature, -1), prefe...]
    gather x9 -> x0, local copies, waits for them, and re-layouts: 17.1 us -> none  [the longest x1 6.96 us: attend_projected(): projected[jnp.arange(copies)[:, None], positions, :, 0]]
    dot_general x1 -> x0, local copies, waits for them, and re-layouts: 15.1 us -> none  [on_device(): jnp.dot(normed.reshape(-1, feature), qkv_part.reshape(feature, -1), prefe...]
    all_gather x1 -> x0, blocking collectives: 12.8 us -> none  [on_device(): everything = lax.all_gather(attention_logits, 'dp', axis=0, tiled=True)]
    reduce_sum x9 -> x0, other arithmetic: 6.93 us -> none  [the longest x2 3.26 us: layer_norm(): average = jnp.mean(inputs, axis=-1, keepdims=True)]
    reshape x0 -> x3, local copies, waits for them, and re-layouts: none -> 6.64 us  [the longest x1 4.07 us: on_device(): weight = jnp.swapaxes(w_qkv.reshape(feature, chunks, width), 0, 1)]
  transfers between devices with their start and end apart: 3 -> 0, of which waited for: 2 -> 0; matrix products, arithmetic and copies ran while one was open for 35% -> 0% of each run, Pallas kernels for 0% -> 0%
where the time goes in v1:
time: 75.1 us; the launch traced here: 74.7 us
  Pallas kernels  64 us (85%)
  local copies, waits for them, and re-layouts  10.7 us (14%)
    pallas_call x1, Pallas kernels, on_device(): pl.pallas_call(functools.partial(kernel, (n_dp, n_mp, head_size, in_chunk...  64 us
    reshape x1, local copies, waits for them, and re-layouts, on_device(): weight = jnp.swapaxes(w_qkv.reshape(feature, chunks, width), 0, 1)  4.07 us
    unnamed x3, local copies, waits for them, and re-layouts  1.81 us

profile of v1, /device:TPU:0, one launch (start us, length us, event | category | flops | bytes accessed | tf_op | source)
XLA Modules:
  0.0 74.7 jit_solution(4490824655565986350)
XLA Ops:
  0.0 1.3 %reshape.22.gain_ref = f32[1,1280]{1,0:T(1,128)} reshape(f32[1280]{0:T(1024)} %param.16) | data formatting | bytes 10240 | tf_op jit(solution)/shard_map/reshape | solution.py:470
  1.3 1.3 %reshape.23.final_gain_ref = f32[1,1280]{1,0:T(1,128)} reshape(f32[1280]{0:T(1024)} %param.19) | data formatting | bytes 10240 | tf_op jit(solution)/shard_map/reshape | solution.py:471
  2.6 1.8 %copy.20.decoder_ref = bf16[1280,33]{1,0:T(8,128)(2,1)} copy(bf16[1280,33]{0,1:T(8,128)(2,1)} %param.21) | data formatting | bytes 168960 | tf_op args[6]
  4.4 0.0 copy-start
  4.4 4.1 %copy.18 = bf16[1280,2,384]{2,0,1:T(8,128)(2,1)} copy(bf16[1280,2,384]{0,2,1:T(8,128)(2,1)} %bitcast.9) | data formatting | bytes 3932160 | tf_op jit(solution)/shard_map/reshape | solution.py:427
  8.5 0.0 copy-done
  8.5 0.9 %copy.19 = bf16[4,64,1280]{2,1,0:T(8,128)(2,1)} copy(bf16[4,64,1280]{2,0,1:T(4,128)(2,1)S(1)} %bitcast.11) | data formatting | bytes 1310720 | tf_op jit(solution)/shard_map/transpose | solution.py:428
  9.4 64.0 %score_copies.1 = f32[4,128]{1,0:T(4,128)} custom-call(s32[32]{0:T(128)} %sequence_ref.1, s32[24]{0:T(128)} %lengths_ref.1, s32[32,64]{1,0:T(8,128)} %codes_ref.1, s32[24,640]{1,0:T(8,128)} %tokens_ref.1, s32[1,32]{1,0:T(1,128)} %bitcast.12, f32[1,1280]{1,0:T(1,128)} %reshape.22.gain_ref, f32[1,1280]{1,0:T(1,128)} %reshape.23.final_gain_ref, ...), custom_call_target="tpu_custom_call" | custom-call | tf_op jit(solution)/shard_map/score_copies/pallas_call | solution.py:436
  73.4 1.3 %constant_dynamic-slice_fusion = f32[4,16]{1,0:T(4,128)} fusion(f32[4,128]{1,0:T(4,128)} %score_copies.1, s32[]{:T(128)S(6)} %select_n.3), kind=kLoop, calls=%fused_computation | loop fusion | bytes 516 | tf_op jit(solution)/shard_map/dynamic_slice | solution.py:482
Async XLA Ops:
  4.4 4.1 %copy-start = (bf16[64,4,1280]{2,1,0:T(4,128)(2,1)S(1)}, bf16[64,4,1280]{2,1,0:T(4,128)(2,1)}, u32[]{:S(2)}) copy-start(bf16[64,4,1280]{2,1,0:T(4,128)(2,1)} %param.18) | copy-start | bytes 1966084

commit v2 on v1

--- a/solution.py
+++ b/solution.py
@@ -78,6 +78,7 @@
     local_sem,
     direct_sem,
     relay_sem,
+    exchange_sem,
     share_sem,
     arrive_sem,
     shared_sem,
@@ -93,8 +94,7 @@
     me = dp * n_mp + mp
     seq_span, feature = hidden.shape
     masks = codes_ref.shape[1]
-    chunk_rows = chunk_heads = heads_in_chunk * head_size
-    half_rows = feature // 2
+    chunk_heads = heads_in_chunk * head_size
     out_rows = obuf.shape[1]
     piece_rows = out_rows // 4
 
@@ -121,18 +121,27 @@
 
     lax.fori_loop(1, devices, greet, 0)
 
+    parity = (dp // 2) % 2
+    above = dp + 2 - 4 * parity
+    part_rows = wbuf.shape[2] // 4
+
+    def part(chunk, odd):
+        return 2 * chunk + odd
+
+    def place(relation, item, half):
+        if item < 2 * chunks:
+            chunk, odd = divmod(item, 2)
+            which = 1 - parity if odd else parity
+            start = (2 * half + which) * part_rows
+            return wbuf.at[relation, chunk, pl.ds(pl.multiple_of(start, 16), part_rows), :]
+        start = (2 * half + item - 2 * chunks) * piece_rows
+        return obuf.at[relation, pl.ds(pl.multiple_of(start, 16), piece_rows), :]
+
     def view(relation, item):
-        if item < chunks:
-            return wbuf.at[relation, item, pl.ds(pl.multiple_of(core * half_rows, 16), half_rows), :]
-        start = core * (2 * piece_rows) + (item - chunks) * piece_rows
-        return obuf.at[relation, pl.ds(pl.multiple_of(start, 16), piece_rows), :]
+        return place(relation, item, core)
 
     def partner_view(relation, item):
-        if item < chunks:
-            start = (1 - core) * half_rows
-            return wbuf.at[relation, item, pl.ds(pl.multiple_of(start, 16), half_rows), :]
-        start = (1 - core) * (2 * piece_rows) + (item - chunks) * piece_rows
-        return obuf.at[relation, pl.ds(pl.multiple_of(start, 16), piece_rows), :]
+        return place(relation, item, 1 - core)
 
     sent = []
 
@@ -153,6 +162,18 @@
 
     def relay(target, source_relation, item):
         to_group(target, source_relation, source_relation ^ target, item, relay_sem.at[item])
+
+    def exchange(relation, chunk):
+        copy = pltpu.make_async_remote_copy(
+            src_ref=view(relation, part(chunk, 0)),
+            dst_ref=view(relation, part(chunk, 0)),
+            send_sem=exchange_sem.at[relation, chunk],
+            recv_sem=arrive_sem.at[relation, part(chunk, 1)],
+            device_id=(above, mp),
+            device_id_type=MESH,
+        )
+        copy.start()
+        sent.append(copy)
 
     def arrived(relation, item):
         landing = view(relation, item)
@@ -196,13 +217,13 @@
     weight_copy.wait()
     out_weight_copy.wait()
     pl.semaphore_wait(barrier, devices - 1)
-    items = chunks + 2
-    routed = n_mp == 4 and chunks == 2
+    items = 2 * chunks + 2
+    routed = n_mp == 4 and chunks == 2 and n_dp % 4 == 0
     if routed:
-        direct(1, 0)
-        direct(2, 1)
-        direct(1, 1)
-        direct(2, 0)
+        direct(1, part(1, 0))
+        direct(2, part(0, 0))
+        direct(1, part(0, 0))
+        direct(2, part(1, 0))
     else:
         for item in range(items):
             for target in range(1, n_mp):
@@ -213,7 +234,7 @@
 
     def norm_rows(step, carry):
         rows = pl.ds(pl.multiple_of(step * tile, tile), tile)
-        normed[rows, :] = (layer_norm(hidden[rows, :].astype(f32)) * gain_ref[...]).astype(bf16)
+        normed[rows, :] = (layer_norm(hidden[rows, :].astype(f32)) * gain_ref[...].reshape(1, feature)).astype(bf16)
         return carry
 
     lax.fori_loop(0, seq_span // tile, norm_rows, 0)
@@ -236,7 +257,8 @@
         )
         return inputs * cosine + turned * sine
 
-    width = wbuf.shape[3]
+    width = wbuf.shape[2]
+    transposed = (((1,), (1,)), ((), ()))
     span = seq_span // 2 if seq_span % 32 == 0 else seq_span
 
     def attend(relation, chunk):
@@ -244,7 +266,7 @@
 
         def project(step, carry):
             rows = pl.ds(pl.multiple_of(step * span, 16), span)
-            made = jnp.dot(normed[rows, :], weights[...], preferred_element_type=f32)
+            made = lax.dot_general(normed[rows, :], weights[...], transposed, preferred_element_type=f32)
             for start in range(0, width, LANES):
                 end = min(start + LANES, width)
                 part = made[:, start:end]
@@ -262,7 +284,8 @@
             return carry
 
         lax.fori_loop(0, seq_span // span, project, 0)
-        made = jnp.dot(masked_rows, weights[...], preferred_element_type=f32) * head_size ** (-0.5)
+        made = lax.dot_general(masked_rows, weights[...], transposed, preferred_element_type=f32)
+        made = made * head_size ** (-0.5)
         total = None
         for head in range(heads_in_chunk):
             at = head * 3 * head_size
@@ -276,7 +299,7 @@
             logits = lax.dot_general(
                 query,
                 pbuf[:, block : block + LANES],
-                (((1,), (1,)), ((), ())),
+                transposed,
                 preferred_element_type=f32,
             )
             logits = jnp.where(alive, logits, -1e30)
@@ -301,58 +324,83 @@
                 context[relation, chunk], obuf[relation, rows, :], preferred_element_type=f32
             )
 
-    def attend_all(pairs):
-        for relation, chunk in pairs:
-            attend(relation, chunk)
-
-    attend_all([(0, chunk) for chunk in range(chunks)])
-    mix(0)
-
-    def fetch(pairs, relays=()):
+    def fetch(*pairs):
         for pair in pairs:
             arrived(*pair)
-            for target, source_relation, item in relays:
-                if (source_relation, item) == pair:
-                    relay(target, source_relation, item)
             share(*pair)
 
+    def attend_shared(relation, chunk):
+        was_shared(relation, part(chunk, 0))
+        was_shared(relation, part(chunk, 1))
+        attend(relation, chunk)
+
+    attend(0, 0)
     if routed:
-        relays = [(1, 2, 1), (2, 1, 0), (1, 2, chunks + 1), (2, 1, chunks)]
-        fetch([(1, 0), (2, 1)], relays)
-        for item in (chunks, chunks + 1):
-            direct(1, 2 * chunks + 1 - item)
-            direct(2, item)
-        for pair in [(1, 0), (2, 1)]:
-            was_shared(*pair)
-            attend(*pair)
-        fetch([(1, 1), (2, 0)], relays)
-        for pair in [(1, 1), (2, 0)]:
-            was_shared(*pair)
-            attend(*pair)
-        fetch([(3, 0), (3, 1)])
-        for pair in [(3, 0), (3, 1)]:
-            was_shared(*pair)
-            attend(*pair)
-        fetch([(1, chunks), (2, chunks + 1), (1, chunks + 1), (2, chunks)], relays)
-        fetch([(3, chunks), (3, chunks + 1)])
-        for relation in (1, 2, 3):
-            was_shared(relation, chunks)
-            was_shared(relation, chunks + 1)
+        first_piece, second_piece = 2 * chunks, 2 * chunks + 1
+        arrived(1, part(1, 0))
+        relay(2, 1, part(1, 0))
+        exchange(1, 1)
+        share(1, part(1, 0))
+        arrived(2, part(0, 0))
+        relay(1, 2, part(0, 0))
+        exchange(2, 0)
+        share(2, part(0, 0))
+        direct(1, part(0, 1))
+        direct(2, part(1, 1))
+        direct(1, first_piece)
+        direct(2, second_piece)
+        direct(1, second_piece)
+        direct(2, first_piece)
+    for chunk in range(1, chunks):
+        attend(0, chunk)
+    mix(0)
+    if routed:
+        fetch((1, part(0, 0)), (2, part(1, 0)), (1, part(1, 1)))
+        arrived(3, part(0, 0))
+        exchange(3, 0)
+        share(3, part(0, 0))
+        arrived(3, part(1, 0))
+        exchange(3, 1)
+        share(3, part(1, 0))
+        fetch((2, part(0, 1)))
+        attend_shared(1, 1)
+        attend_shared(2, 0)
+        fetch((1, part(0, 1)), (2, part(1, 1)), (3, part(0, 1)))
+        attend_shared(1, 0)
+        arrived(1, first_piece)
+        relay(2, 1, first_piece)
+        share(1, first_piece)
+        arrived(2, second_piece)
+        relay(1, 2, second_piece)
+        share(2, second_piece)
+        attend_shared(2, 1)
+        fetch((3, part(1, 1)))
+        attend_shared(3, 0)
+        fetch((1, second_piece), (2, first_piece))
+        attend_shared(3, 1)
+        for relation in (1, 2):
+            was_shared(relation, first_piece)
+            was_shared(relation, second_piece)
             mix(relation)
+        fetch((3, first_piece), (3, second_piece))
+        was_shared(3, first_piece)
+        was_shared(3, second_piece)
+        mix(3)
     else:
         for relation in range(1, n_mp):
-            fetch([(relation, item) for item in range(items)])
+            fetch(*[(relation, item) for item in range(items)])
         for relation in range(1, n_mp):
             for item in range(items):
                 was_shared(relation, item)
-            attend_all([(relation, chunk) for chunk in range(chunks)])
+            for chunk in range(chunks):
+                attend(relation, chunk)
             mix(relation)
 
-    normed_final = (layer_norm(mixed[...]) * final_gain_ref[...]).astype(bf16)
+    normed_final = (layer_norm(mixed[...]) * final_gain_ref[...].reshape(1, feature)).astype(bf16)
     dense_copy.wait()
     dense_out = jnp.dot(normed_final, dense[...], preferred_element_type=f32)
     headed = layer_norm(0.5 * dense_out * (1.0 + lax.erf(dense_out * 0.5**0.5))).astype(bf16)
-    logits = jnp.dot(headed, decoder_ref[...], preferred_element_type=f32) + bias_ref[...]
+    logits = lax.dot_general(headed, decoder_ref[...], transposed, preferred_element_type=f32) + bias_ref[...]
     largest = jnp.max(logits, axis=-1, keepdims=True)
     scale = jnp.log(jnp.sum(jnp.exp(logits - largest), axis=-1, keepdims=True)) + largest
     vocabulary = lax.broadcasted_iota(jnp.int32, logits.shape, 1).astype(f32)
@@ -424,11 +472,11 @@
     in_chunk = 2 if heads % 2 == 0 else 1
     chunks = heads // in_chunk
     width = in_chunk * 3 * head_size
-    weight = jnp.swapaxes(w_qkv.reshape(feature, chunks, width), 0, 1)
+    weight = jnp.transpose(w_qkv.reshape(feature, chunks, width), (1, 2, 0))
     out_weight = jnp.swapaxes(output_weight, 0, 1).reshape(heads * head_size, feature)
     cosine, sine = rotary_tables(seq_span, head_size)
     group = copies // n_dp
-    items = chunks + 2
+    items = 2 * chunks + 2
     dma = pltpu.SemaphoreType.DMA
     vmem = pl.BlockSpec(memory_space=pltpu.VMEM)
     smem = pl.BlockSpec(memory_space=pltpu.SMEM)
@@ -442,7 +490,7 @@
         scratch_shapes=[
             pltpu.VMEM((seq_span, feature), bf16),
             pltpu.VMEM((seq_span, feature), bf16),
-            pltpu.VMEM((n_mp, chunks, feature, width), bf16),
+            pltpu.VMEM((n_mp, chunks, width, feature), bf16),
             pltpu.VMEM((n_mp, heads * head_size, feature), bf16),
             pltpu.VMEM((feature, feature), bf16),
             pltpu.VMEM((seq_span, LANES), f32),
@@ -454,6 +502,7 @@
             dma((6,)),
             dma((n_mp, items)),
             dma((items,)),
+            dma((n_mp, chunks)),
             dma((n_mp, items)),
             dma((n_mp, items)),
             dma((n_mp, items)),
@@ -467,9 +516,9 @@
         mask_code,
         seq_tokens,
         copy_owner.reshape(1, -1),
-        ln_attn_gain.reshape(1, -1),
-        ln_final_gain.reshape(1, -1),
-        decoder_weight,
+        ln_attn_gain,
+        ln_final_gain,
+        decoder_weight.T,
         decoder_bias.reshape(1, -1),
         hidden_states.reshape(seq_span, feature),
         weight,

time: 75.1 us -> 60.6 us (0.81)
  local copies, waits for them, and re-layouts: 10.7 us -> 3.27 us
  Pallas kernels: 64 us -> 57.1 us
    pallas_call x1, Pallas kernels: 64 us -> 57.1 us  [on_device(): pl.pallas_call(functools.partial(kernel, (n_dp, n_mp, head_size, in_chunk...]
    reshape x3 -> x0, local copies, waits for them, and re-layouts: 6.64 us -> none  [the longest x1 4.07 us: on_device(): weight = jnp.swapaxes(w_qkv.reshape(feature, chunks, width), 0, 1)]
    unnamed x3 -> x0, local copies, waits for them, and re-layouts: 1.81 us -> none
    transpose x1, local copies, waits for them, and re-layouts: 0.91 us -> 1.99 us  [on_device(): jnp.swapaxes(output_weight, 0, 1).reshape(heads * head_size, feature)]
where the time goes in v2:
time: 60.6 us; the launch traced here: 60.3 us
  Pallas kernels  57.1 us (94%)
  local copies, waits for them, and re-layouts  3.27 us (5%)
    pallas_call x1, Pallas kernels, on_device(): pl.pallas_call(functools.partial(kernel, (n_dp, n_mp, head_size, in_chunk...  57.1 us
    transpose x1, local copies, waits for them, and re-layouts, on_device(): jnp.swapaxes(output_weight, 0, 1).reshape(heads * head_size, feature)  1.99 us
    dynamic_slice x1, local copies, waits for them, and re-layouts, on_device(): return lax.dynamic_slice_in_dim(rows, lax.axis_index('mp') * own, own, 1)  1.29 us

profile of v2, /device:TPU:0, one launch (start us, length us, event | category | flops | bytes accessed | tf_op | source)
XLA Modules:
  0.0 60.3 jit_solution(7814675357178965878)
XLA Ops:
  0.0 2.0 %copy.16 = bf16[4,64,1280]{2,1,0:T(8,128)(2,1)} copy(bf16[4,64,1280]{2,0,1:T(4,128)(2,1)} %bitcast.12) | data formatting | bytes 1310720 | tf_op jit(solution)/shard_map/transpose | solution.py:476
  2.0 57.1 %score_copies.1 = f32[4,128]{1,0:T(4,128)} custom-call(s32[32]{0:T(128)} %sequence_ref.1, s32[24]{0:T(128)} %lengths_ref.1, s32[32,64]{1,0:T(8,128)} %codes_ref.1, s32[24,640]{1,0:T(8,128)} %tokens_ref.1, s32[1,32]{1,0:T(1,128)} %bitcast.14, f32[1280]{0:T(1024)} %gain_ref.1, f32[1280]{0:T(1024)} %final_gain_ref.1, bf16[33,1280]{1,0:T(8,128)(2,1)} %bitcast.13, ...), custom_call_target="tpu_custom_call" | custom-call | tf_op jit(solution)/shard_map/score_copies/pallas_call | solution.py:484
  59.1 1.3 %constant_dynamic-slice_fusion = f32[4,16]{1,0:T(4,128)} fusion(f32[4,128]{1,0:T(4,128)} %score_copies.1, s32[]{:T(128)S(6)} %select_n.3), kind=kLoop, calls=%fused_computation | loop fusion | bytes 516 | tf_op jit(solution)/shard_map/dynamic_slice | solution.py:531

commit v3 on v2

--- a/solution.py
+++ b/solution.py
@@ -257,65 +257,53 @@
         )
         return inputs * cosine + turned * sine
 
-    width = wbuf.shape[2]
     transposed = (((1,), (1,)), ((), ()))
+    low = lane < head_size
     span = seq_span // 2 if seq_span % 32 == 0 else seq_span
+    head_rows = 3 * head_size
 
     def attend(relation, chunk):
         weights = wbuf.at[relation, chunk]
+        pairs = [
+            weights[head * head_rows + head_size : (head + 1) * head_rows, :]
+            for head in range(heads_in_chunk)
+        ]
+        pair_weights = pairs[0] if heads_in_chunk == 1 else jnp.concatenate(pairs, axis=0)
 
         def project(step, carry):
             rows = pl.ds(pl.multiple_of(step * span, 16), span)
-            made = lax.dot_general(normed[rows, :], weights[...], transposed, preferred_element_type=f32)
-            for start in range(0, width, LANES):
-                end = min(start + LANES, width)
-                part = made[:, start:end]
-                keys = [
-                    head * 3 * head_size + head_size
-                    for head in range(heads_in_chunk)
-                    if start <= head * 3 * head_size + head_size < end
-                ]
-                for key in keys:
-                    low = key - start
-                    turned = rotate(part, cos[rows, :], sin[rows, :])
-                    inside = (lane >= low) & (lane < low + head_size)
-                    part = jnp.where(inside, turned, part)
-                pbuf[rows, start:end] = part.astype(bf16)
+            made = lax.dot_general(
+                normed[rows, :], pair_weights, transposed, preferred_element_type=f32
+            )
+            for head in range(heads_in_chunk):
+                block = made[:, head * LANES : (head + 1) * LANES]
+                block = jnp.where(low, rotate(block, cos[rows, :], sin[rows, :]), block)
+                pbuf[rows, head * LANES : (head + 1) * LANES] = block.astype(bf16)
             return carry
 
         lax.fori_loop(0, seq_span // span, project, 0)
-        made = lax.dot_general(masked_rows, weights[...], transposed, preferred_element_type=f32)
-        made = made * head_size ** (-0.5)
-        total = None
+        if heads_in_chunk == 1:
+            query_weights = weights[: 2 * head_size, :]
+        else:
+            query_weights = jnp.concatenate(
+                [weights[:head_size, :], weights[head_rows : head_rows + head_size, :]], axis=0
+            )
+        made = lax.dot_general(masked_rows, query_weights, transposed, preferred_element_type=f32)
+        turned = rotate(made * head_size ** (-0.5), query_cos, query_sin)
+        vectors = []
         for head in range(heads_in_chunk):
-            at = head * 3 * head_size
-            block = at // LANES * LANES
-            query = rotate(made[:, block : block + LANES], query_cos, query_sin)
-            query = pltpu.roll(query, head_size, 1)
-            key = at + head_size
-            block = key // LANES * LANES
-            inside = (lane >= key - block) & (lane < key - block + head_size)
-            query = jnp.where(inside, query, 0.0).astype(bf16)
-            logits = lax.dot_general(
-                query,
-                pbuf[:, block : block + LANES],
-                transposed,
-                preferred_element_type=f32,
-            )
+            query = turned if head == 0 else pltpu.roll(turned, head_size, 1)
+            query = jnp.where(low, query, 0.0).astype(bf16)
+            block = pbuf[:, head * LANES : (head + 1) * LANES]
+            logits = lax.dot_general(query, block, transposed, preferred_element_type=f32)
             logits = jnp.where(alive, logits, -1e30)
             weight = jnp.exp(logits - jnp.max(logits, axis=-1, keepdims=True))
             probs = (weight / jnp.sum(weight, axis=-1, keepdims=True)).astype(bf16)
-            value = at + 2 * head_size
-            block = value // LANES * LANES
-            end = min(block + LANES, width)
-            vectors = jnp.dot(probs, pbuf[:, block:end], preferred_element_type=f32)
-            if total is None:
-                total = vectors
-            else:
-                low = value - block
-                inside = (lane >= low) & (lane < low + head_size)
-                total = jnp.where(inside, vectors, total)
-        context[relation, chunk] = total.astype(bf16)
+            vectors.append(jnp.dot(probs, block, preferred_element_type=f32))
+        total = pltpu.roll(vectors[0], head_size, 1)
+        if heads_in_chunk > 1:
+            total = jnp.where(low, total, vectors[1])
+        context[relation, chunk] = total[:, :chunk_heads].astype(bf16)
 
     def mix(relation):
         for chunk in range(chunks):
@@ -406,14 +394,14 @@
     vocabulary = lax.broadcasted_iota(jnp.int32, logits.shape, 1).astype(f32)
     picked = jnp.sum(jnp.where(vocabulary == targets, logits - scale, 0.0), axis=1, keepdims=True)
     row = jnp.sum(jnp.where(eye, picked, 0.0), axis=0, keepdims=True)
-    padded = jnp.concatenate([row, jnp.zeros((1, LANES - masks), f32)], axis=1) if masks < LANES else row
+    padded = jnp.pad(row, ((0, 0), (0, LANES - masks)))
     scores[me] = jnp.broadcast_to(padded, scores.shape[1:])
 
     def score_copy(step):
         other = (me + step) % devices
         return pltpu.make_async_remote_copy(
-            src_ref=scores.at[me],
-            dst_ref=scores.at[me],
+            src_ref=scores.at[me, pl.ds(0, 1), :],
+            dst_ref=scores.at[me, pl.ds(0, 1), :],
             send_sem=score_send_sem.at[step],
             recv_sem=score_sem.at[me],
             device_id=(other // n_mp, other % n_mp),
@@ -430,7 +418,7 @@
 
     def wait_scores(step, carry):
         source = (me + step) % devices
-        landing = scores.at[source]
+        landing = scores.at[source, pl.ds(0, 1), :]
         pltpu.make_async_copy(landing, landing, score_sem.at[source]).wait()
         return carry
 
@@ -469,6 +457,7 @@
     head_size, heads, _ = output_weight.shape
     copies, masks = mask_code.shape
     assert lane_copies == 1 and copies == devices and n_dp % 2 == 0
+    assert 2 * head_size == LANES and masks <= LANES
     in_chunk = 2 if heads % 2 == 0 else 1
     chunks = heads // in_chunk
     width = in_chunk * 3 * head_size
@@ -495,7 +484,7 @@
             pltpu.VMEM((feature, feature), bf16),
             pltpu.VMEM((seq_span, LANES), f32),
             pltpu.VMEM((seq_span, LANES), f32),
-            pltpu.VMEM((seq_span, width), bf16),
+            pltpu.VMEM((seq_span, in_chunk * LANES), bf16),
             pltpu.VMEM((n_mp, chunks, masks, in_chunk * head_size), bf16),
             pltpu.VMEM((masks, feature), f32),
             pltpu.VMEM((devices, 8, LANES), f32),

time: 60.6 us -> 57.1 us (0.942)
  Pallas kernels: 57.1 us -> 53.6 us
    pallas_call x1, Pallas kernels: 57.1 us -> 53.6 us  [on_device(): pl.pallas_call(functools.partial(kernel, (n_dp, n_mp, head_size, in_chunk...]
where the time goes in v3:
time: 57.1 us; the launch traced here: 56.8 us
  Pallas kernels  53.6 us (94%)
  local copies, waits for them, and re-layouts  3.27 us (6%)
    pallas_call x1, Pallas kernels, on_device(): pl.pallas_call(functools.partial(kernel, (n_dp, n_mp, head_size, in_chunk...  53.6 us
    transpose x1, local copies, waits for them, and re-layouts, on_device(): jnp.swapaxes(output_weight, 0, 1).reshape(heads * head_size, feature)  1.99 us
    dynamic_slice x1, local copies, waits for them, and re-layouts, on_device(): return lax.dynamic_slice_in_dim(rows, lax.axis_index('mp') * own, own, 1)  1.29 us

profile of v3, /device:TPU:0, one launch (start us, length us, event | category | flops | bytes accessed | tf_op | source)
XLA Modules:
  0.0 56.8 jit_solution(18156202289298131576)
XLA Ops:
  0.0 2.0 %copy.16 = bf16[4,64,1280]{2,1,0:T(8,128)(2,1)} copy(bf16[4,64,1280]{2,0,1:T(4,128)(2,1)} %bitcast.12) | data formatting | bytes 1310720 | tf_op jit(solution)/shard_map/transpose | solution.py:465
  2.0 53.6 %score_copies.1 = f32[4,128]{1,0:T(4,128)} custom-call(s32[32]{0:T(128)} %sequence_ref.1, s32[24]{0:T(128)} %lengths_ref.1, s32[32,64]{1,0:T(8,128)} %codes_ref.1, s32[24,640]{1,0:T(8,128)} %tokens_ref.1, s32[1,32]{1,0:T(1,128)} %bitcast.14, f32[1280]{0:T(1024)} %gain_ref.1, f32[1280]{0:T(1024)} %final_gain_ref.1, bf16[33,1280]{1,0:T(8,128)(2,1)} %bitcast.13, ...), custom_call_target="tpu_custom_call" | custom-call | tf_op jit(solution)/shard_map/score_copies/pallas_call | solution.py:473
  55.6 1.3 %constant_dynamic-slice_fusion = f32[4,16]{1,0:T(4,128)} fusion(f32[4,128]{1,0:T(4,128)} %score_copies.1, s32[]{:T(128)S(6)} %select_n.3), kind=kLoop, calls=%fused_computation | loop fusion | bytes 516 | tf_op jit(solution)/shard_map/dynamic_slice | solution.py:520

commit v4 on v3

--- a/solution.py
+++ b/solution.py
@@ -103,12 +103,8 @@
         copy.start()
         return copy
 
+    weight_copy = local(1, weight_hbm, wbuf.at[0])
     hidden_copy = local(0, hidden_hbm, hidden)
-    weight_copy = local(1, weight_hbm, wbuf.at[0])
-    out_weight_copy = local(2, out_weight_hbm, obuf.at[0])
-    cos_copy = local(3, cos_hbm, cos)
-    sin_copy = local(4, sin_hbm, sin)
-    dense_copy = local(5, dense_hbm, dense)
 
     barrier = pltpu.get_barrier_semaphore()
 
@@ -215,7 +211,6 @@
     alive = lax.broadcasted_iota(jnp.int32, (1, seq_span), 1).astype(f32) < length
 
     weight_copy.wait()
-    out_weight_copy.wait()
     pl.semaphore_wait(barrier, devices - 1)
     items = 2 * chunks + 2
     routed = n_mp == 4 and chunks == 2 and n_dp % 4 == 0
@@ -224,7 +219,12 @@
         direct(2, part(0, 0))
         direct(1, part(0, 0))
         direct(2, part(1, 0))
-    else:
+    cos_copy = local(3, cos_hbm, cos)
+    sin_copy = local(4, sin_hbm, sin)
+    out_weight_copy = local(2, out_weight_hbm, obuf.at[0])
+    dense_copy = local(5, dense_hbm, dense)
+    if not routed:
+        out_weight_copy.wait()
         for item in range(items):
             for target in range(1, n_mp):
                 direct(target, item)
@@ -335,6 +335,7 @@
         share(2, part(0, 0))
         direct(1, part(0, 1))
         direct(2, part(1, 1))
+        out_weight_copy.wait()
         direct(1, first_piece)
         direct(2, second_piece)
         direct(1, second_piece)

time: 57.1 us -> 57 us (level)
  no operation moved by 1% of the time
where the time goes in v4:
time: 57 us; the launch traced here: 56.8 us
  Pallas kernels  53.5 us (94%)
  local copies, waits for them, and re-layouts  3.27 us (6%)
    pallas_call x1, Pallas kernels, on_device(): pl.pallas_call(functools.partial(kernel, (n_dp, n_mp, head_size, in_chunk...  53.5 us
    transpose x1, local copies, waits for them, and re-layouts, on_device(): jnp.swapaxes(output_weight, 0, 1).reshape(heads * head_size, feature)  1.99 us
    dynamic_slice x1, local copies, waits for them, and re-layouts, on_device(): return lax.dynamic_slice_in_dim(rows, lax.axis_index('mp') * own, own, 1)  1.29 us

profile of v4, /device:TPU:0, one launch (start us, length us, event | category | flops | bytes accessed | tf_op | source)
XLA Modules:
  0.0 56.8 jit_solution(14298764764992810529)
XLA Ops:
  0.0 2.0 %copy.16 = bf16[4,64,1280]{2,1,0:T(8,128)(2,1)} copy(bf16[4,64,1280]{2,0,1:T(4,128)(2,1)} %bitcast.12) | data formatting | bytes 1310720 | tf_op jit(solution)/shard_map/transpose | solution.py:466
  2.0 53.5 %score_copies.1 = f32[4,128]{1,0:T(4,128)} custom-call(s32[32]{0:T(128)} %sequence_ref.1, s32[24]{0:T(128)} %lengths_ref.1, s32[32,64]{1,0:T(8,128)} %codes_ref.1, s32[24,640]{1,0:T(8,128)} %tokens_ref.1, s32[1,32]{1,0:T(1,128)} %bitcast.14, f32[1280]{0:T(1024)} %gain_ref.1, f32[1280]{0:T(1024)} %final_gain_ref.1, bf16[33,1280]{1,0:T(8,128)(2,1)} %bitcast.13, ...), custom_call_target="tpu_custom_call" | custom-call | tf_op jit(solution)/shard_map/score_copies/pallas_call | solution.py:474
  55.5 1.3 %constant_dynamic-slice_fusion = f32[4,16]{1,0:T(4,128)} fusion(f32[4,128]{1,0:T(4,128)} %score_copies.1, s32[]{:T(128)S(6)} %select_n.3), kind=kLoop, calls=%fused_computation | loop fusion | bytes 516 | tf_op jit(solution)/shard_map/dynamic_slice | solution.py:521
